TPU v7x, 512 devices: a 8x2x16 block of a 8x8x16 slice. The times are simulated.
512 devices in a mesh: slab: 2 (over y), date: 16 (over z), tile: 8 (over x), sub: 2 (over core).
Axes of the slice: x: 8, y: 2, z: 16, core: 2. Of those that a mesh axis runs over, the one named last changes fastest.
The devices are a block of a 8x8x16 slice.
Arguments:
- slc: bfloat16 [2, 100, 128, 8192], P(None, None, 'date', ('slab', 'tile', 'sub')), parts along dimension 3, may hold values from -300 to 300, as said below
- usable: int32 [100, 128, 8192], P(None, 'date', ('slab', 'tile', 'sub')), parts along dimension 2, may hold values 0 or 1
Outputs:
- coherence: bfloat16 [2, 32, 16, 16, 128, 128], P(None, ('slab', 'tile', 'sub'), 'date'), parts along dimension 1
- linked: float32 [2, 128, 8192], P(None, 'date', ('slab', 'tile', 'sub')), parts along dimension 2
There are 2 independent parts, one for each index of `slab`. A program takes and returns all parts, laid end to end along the dimension named above; each array names one. Nothing has to cross between parts.
Inputs may be any that keep to these rules, and one draw needn't show every extreme that they name: `slc`: complex samples of a partly coherent stack.
All inputs are finite; a program needn't handle non-finite values. No bound on the sum of `usable` on one device may be relied on, other than what follows from the above.
Results may differ from a plain program's by a relative error of at most 0.0016.
Values may be sent and summed in bfloat16 or wider, within the bound.
A program may use at most 64 MiB of HBM per device.

v0:
```python
import jax
import jax.numpy as jnp
from jax import lax
from jax.sharding import PartitionSpec as P

ITERS = 4


def inverse_roots(block):
    samples = block.astype(jnp.float32)
    intensity = jnp.mean(samples[0] * samples[0] + samples[1] * samples[1], axis=0) + 1e-05
    return lax.rsqrt(intensity)


def pair_terms(left_block, right_block, left_root, right_root, looks_count):
    real_sum = jnp.einsum(
        "law,lbw->wab", left_block[0], right_block[0], preferred_element_type=jnp.float32
    )
    real_sum = real_sum + jnp.einsum(
        "law,lbw->wab", left_block[1], right_block[1], preferred_element_type=jnp.float32
    )
    imag_sum = jnp.einsum(
        "law,lbw->wab", left_block[1], right_block[0], preferred_element_type=jnp.float32
    )
    imag_sum = imag_sum - jnp.einsum(
        "law,lbw->wab", left_block[0], right_block[1], preferred_element_type=jnp.float32
    )
    factor = left_root.T[:, :, None] * right_root.T[:, None, :] * (1.0 / looks_count)
    return jnp.stack([real_sum * factor, imag_sum * factor])


def local_pairs(samples, looks_count):
    window_root = inverse_roots(samples)
    return pair_terms(samples, samples, window_root, window_root, looks_count).astype(jnp.bfloat16)


def complex_apply(matrix, vec_real, vec_imag):
    rr = jnp.einsum("wab,bw->aw", matrix[0], vec_real, precision=lax.Precision.HIGHEST)
    ii = jnp.einsum("wab,bw->aw", matrix[1], vec_imag, precision=lax.Precision.HIGHEST)
    ri = jnp.einsum("wab,bw->aw", matrix[0], vec_imag, precision=lax.Precision.HIGHEST)
    ir = jnp.einsum("wab,bw->aw", matrix[1], vec_real, precision=lax.Precision.HIGHEST)
    return (rr - ii, ri + ir)


def local(slc, usable):
    masked = slc * usable.astype(jnp.bfloat16)[None]
    looks_count = slc.shape[1]
    own_dates = slc.shape[2]
    windows = slc.shape[3]
    blocks_count = lax.axis_size("date")
    all_dates = own_dates * blocks_count
    per_device = windows // blocks_count
    split_view = masked.reshape(2, looks_count, own_dates, blocks_count, per_device)
    result = local_pairs(
        lax.all_to_all(split_view, "date", split_axis=3, concat_axis=2, tiled=True)[:, :, :, 0, :],
        looks_count,
    )
    matrix = result.astype(jnp.float32)
    vec_real = jnp.ones((all_dates, per_device), jnp.float32)
    vec_imag = jnp.zeros((all_dates, per_device), jnp.float32)
    for step in range(ITERS):
        new_real, new_imag = complex_apply(matrix, vec_real, vec_imag)
        scale = lax.rsqrt(jnp.mean(new_real * new_real + new_imag * new_imag, axis=0) + 1e-05)
        vec_real = new_real * scale[None]
        vec_imag = new_imag * scale[None]
    linked = lax.all_to_all(
        jnp.stack([vec_real, vec_imag]), "date", split_axis=1, concat_axis=2, tiled=True
    )
    return (result.reshape(2, 1, 1, per_device, all_dates, all_dates), linked)


def solution(mesh):
    return jax.shard_map(
        local,
        mesh=mesh,
        in_specs=(
            P(None, None, "date", ("slab", "tile", "sub")),
            P(None, "date", ("slab", "tile", "sub")),
        ),
        out_specs=(
            P(None, ("slab", "tile", "sub"), "date", None, None, None),
            P(None, "date", ("slab", "tile", "sub")),
        ),
        check_vma=False,
    )
```

profile of v0, /device:TPU:65, one launch (start us, length us, event | category | flops | bytes accessed | tf_op | source)
XLA Modules:
  0.0 139.3 jit_solution(16312942957457335373)
XLA Ops:
  0.6 1.9 %copy.53 = bf16[2,100,8,256]{1,3,2,0:T(8,128)(2,1)S(1)} copy(bf16[2,100,8,256]{3,2,1,0:T(8,128)(2,1)} %param.2) | data formatting | bytes 1638400 | tf_op args[0]
  3.5 89.3 %all_to_all.33 = bf16[2,100,8,16,16]{1,4,2,0,3:T(8,128)(2,1)S(1)} all-to-all(bf16[2,100,8,16,16]{1,4,2,0,3:T(8,128)(2,1)S(1)} %copy.54), channel_id=1, replica_groups=mesh['slab'=2,'date'=16,'tile'=8,'sub'=2] {'date'}, dimensions={3} | all-to-all | bytes 1638400 | tf_op jit(solution)/shard_map/all_to_all | solution.py:55
  95.7 0.9 fusion.10
  96.7 0.9 fusion.12
  98.5 0.9 fusion.14
  99.4 0.9 fusion.8
  100.5 0.9 fusion.25
  101.4 0.9 fusion.24
  102.4 0.9 fusion.26
  103.3 0.9 fusion.23
  104.4 0.9 fusion.29
  105.4 0.9 fusion.28
  106.3 0.9 fusion.30
  107.2 0.9 fusion.27
  108.4 0.9 fusion.33
  109.3 0.9 fusion.32
  110.2 0.9 fusion.34
  111.1 0.9 fusion.31
  112.4 0.8 reshape.118
  113.2 12.7 %all-to-all-start.1 = ((f32[16,1,256]{2,1,0:T(1,128)}), f32[16,1,256]{2,1,0:T(1,128)S(1)}, u32[]{:S(2)}, u32[]{:S(2)}) async-start(f32[16,1,256]{2,1,0:T(1,128)} %reshape.118), calls=%async_computation.1 | async-start | bytes 32768 | tf_op jit(solution)/shard_map/all_to_all | solution.py:66
  125.9 1.1 pad_maximum_fusion
  127.0 10.1 %all-to-all-done.1 = f32[16,1,256]{2,1,0:T(1,128)S(1)} async-done(((f32[16,1,256]{2,1,0:T(1,128)}), f32[16,1,256]{2,1,0:T(1,128)S(1)}, u32[]{:S(2)}, u32[]{:S(2)}) %all-to-all-start.1) | async-done | bytes 16416 | tf_op jit(solution)/shard_map/all_to_all | solution.py:66
  137.6 0.7 reduce.7
  138.6 0.7 all_to_all.30
  (36 shorter events, 6.4 us)
Async XLA Ops:
  0.6 1.9 %copy-start = (s32[100,8,256]{2,1,0:T(8,128)S(1)}, s32[100,8,256]{2,1,0:T(8,128)}, u32[]{:S(2)}) copy-start(s32[100,8,256]{2,1,0:T(8,128)} %param.3) | copy-start | bytes 2457604
  113.2 23.9 %all-to-all-start.1 = ((f32[16,1,256]{2,1,0:T(1,128)}), f32[16,1,256]{2,1,0:T(1,128)S(1)}, u32[]{:S(2)}, u32[]{:S(2)}) async-start(f32[16,1,256]{2,1,0:T(1,128)} %reshape.118), calls=%async_computation.1 | async-start | bytes 32768 | tf_op jit(solution)/shard_map/all_to_all | solution.py:66
where the time goes:
time: 140 us; the launch traced here: 139 us
  blocking collectives  89.3 us (64%)
  matrix products  16.5 us (12%)
  starting transfers between devices  12.7 us (9%)
  waiting for transfers between devices  10.1 us (7%)
  local copies, waits for them, and re-layouts  6.45 us (5%)
  other arithmetic  3.38 us (2%)
    all_to_all x1, blocking collectives, local(): lax.all_to_all(split_view, 'date', split_axis=3, concat_axis=2, tiled=True)  89.3 us
    all_to_all x1, starting transfers between devices, local(): lax.all_to_all(jnp.stack([vec_real, vec_imag]), 'date', split_axis=1, con...  12.7 us
    all_to_all x1, waiting for transfers between devices, local(): lax.all_to_all(jnp.stack([vec_real, vec_imag]), 'date', split_axis=1, con...  10.1 us
    dot_general x4, matrix products, complex_apply(): jnp.einsum('wab,bw->aw', matrix[1], vec_real, precision=lax.Precision.HIG...  3.7 us
    dot_general x4, matrix products, complex_apply(): jnp.einsum('wab,bw->aw', matrix[0], vec_imag, precision=lax.Precision.HIG...  3.68 us
    dot_general x4, matrix products, complex_apply(): jnp.einsum('wab,bw->aw', matrix[0], vec_real, precision=lax.Precision.HIG...  3.68 us
    dot_general x4, matrix products, complex_apply(): jnp.einsum('wab,bw->aw', matrix[1], vec_imag, precision=lax.Precision.HIG...  3.68 us
    unnamed x5, local copies, waits for them, and re-layouts  2.95 us
  transfers between devices with their start and end apart: 1, of which 1 were waited for; matrix products, arithmetic and copies ran while one was open for 1% of the time, Pallas kernels for 0%

commit v1 on v0

v1 whole, which is shorter than its diff:
```python
import functools

import jax
import jax.numpy as jnp
from jax import lax
from jax.experimental import pallas as pl
from jax.experimental.pallas import tpu as pltpu
from jax.sharding import PartitionSpec as P

ITERS = 4
MESH = pl.DeviceIdType.MESH
F32, BF16 = jnp.float32, jnp.bfloat16
T1, T2 = 16, 8
TILES = T1 + T2 + 1


def lane_iota(shape):
    return lax.broadcasted_iota(jnp.int32, shape, len(shape) - 1)


def pack(slc_ref, usable_ref, plane, split1, split2, send, looks, dates, blocks):
    rows = looks * dates

    def mask_step(l, carry):
        use = usable_ref[l].astype(F32)
        for c in range(2):
            masked = slc_ref[c, l].astype(F32) * use
            at = pl.ds(pl.multiple_of(c * rows + l * dates, 8), dates)
            for half in range(2):
                plane[half, at, :] = masked[:, half * 128:half * 128 + 128]
        return carry

    lax.fori_loop(0, looks, mask_step, 0, unroll=4)

    bit = (lane_iota((8, 8, 128)) // 8) % 2 == 1
    for half in range(2):

        def date_step(a, carry):
            def group(c, look, count):
                return plane[half, pl.ds(c * rows + look * dates + a, count, stride=dates), :]

            first = jnp.concatenate([group(c, 0, 64) for c in range(2)], axis=0)
            split1[pl.ds(half * 1024 + a, 128, stride=8), :] = first.T
            parts = []
            for c in range(2):
                for u in range(4):
                    rest = group(c, 64 + 8 * u, 8)
                    parts += [rest, rest]
            second = jnp.concatenate(parts, axis=0).T.reshape(8, 2, 8, 128)
            pairs = jnp.where(bit, second[:, 0], second[:, 1]).reshape(64, 128)
            split2[pl.ds(half * 512 + a, 64, stride=8), :] = pairs
            return carry

        lax.fori_loop(0, dates, date_step, 0)

    groups = [(c, r) for c in range(2) for r in range(4)]
    for half in range(2):
        left = [plane[half, c * rows + (96 + r) * dates:c * rows + (97 + r) * dates, :] for c, r in groups]
        for b in range(8):
            tile = jnp.zeros((8, 128), F32)
            for g, part in enumerate(left):
                shift = (16 * (g - b)) % 128
                moved = pltpu.roll(part, shift, 1) if shift else part
                tile = jnp.where(lane_iota((8, 128)) // 16 == g, moved, tile)
            send[half * 8 + b, T1 + T2] = tile.astype(BF16)

    def out_step(b, carry):
        one = split1[pl.ds(pl.multiple_of(b * 128, 128), 128), :].reshape(T1, 8, 128)
        two = split2[pl.ds(pl.multiple_of(b * 64, 64), 64), :].reshape(T2, 8, 128)
        send[b, 0:T1] = one.astype(BF16)
        send[b, T1:T1 + T2] = two.astype(BF16)
        return carry

    lax.fori_loop(0, blocks, out_step, 0)


def gram(recv, coherence, i, looks):
    lane = lane_iota((128, 128))
    one = recv[i].astype(F32).reshape(128, 128)
    pair = recv[T1 + i % 8].astype(F32).reshape(128, 128)
    rest = recv[T1 + T2].astype(F32).reshape(128, 128)
    in_pair = ((lane // 8) % 2 == 1) == (i < 8)
    two = jnp.where(in_pair, pair, jnp.where(lane % 16 == i, rest, 0.0))
    sign = jnp.where(lane < 64, 1.0, -1.0)
    plain = jnp.concatenate([one, two], axis=1).astype(BF16)
    turned = jnp.concatenate([pltpu.roll(one, 64, 1) * sign, pltpu.roll(two, 64, 1) * sign], axis=1).astype(BF16)
    both = jnp.concatenate([plain, turned], axis=0)
    cross = lax.dot_general(both, plain, (((1,), (1,)), ((), ())), preferred_element_type=F32)
    real, imag = cross[:128], cross[128:]
    eye = lax.broadcasted_iota(jnp.int32, (128, 128), 0) == lane
    diagonal = jnp.where(eye, real, 0.0)
    column = lax.rsqrt(jnp.sum(diagonal, axis=1, keepdims=True) * (1.0 / looks) + 1e-05)
    row = lax.rsqrt(jnp.sum(diagonal, axis=0, keepdims=True) * (1.0 / looks) + 1e-05)
    factor = column * row * (1.0 / looks)
    coherence[0, 0, 0, i] = (real * factor).astype(BF16)
    coherence[1, 0, 0, i] = (imag * factor).astype(BF16)


def link(coherence, windows):
    vec_real = jnp.ones((windows, 128), F32)
    vec_imag = jnp.zeros((windows, 128), F32)
    row = lax.broadcasted_iota(jnp.int32, (4 * windows, 256), 0) % windows
    for step in range(ITERS):
        high_real, high_imag = vec_real.astype(BF16).astype(F32), vec_imag.astype(BF16).astype(F32)
        low_real, low_imag = vec_real - high_real, vec_imag - high_imag
        lhs = jnp.concatenate(
            [
                jnp.concatenate([high_real, high_imag], axis=1),
                jnp.concatenate([low_real, low_imag], axis=1),
                jnp.concatenate([high_imag, -high_real], axis=1),
                jnp.concatenate([low_imag, -low_real], axis=1),
            ],
            axis=0,
        )
        total = jnp.zeros((4 * windows, 128), F32)
        for w in range(windows):
            stacked = jnp.concatenate([coherence[0, 0, 0, w], coherence[1, 0, 0, w]], axis=0)
            total += jnp.dot(jnp.where(row == w, lhs, 0.0).astype(BF16), stacked, preferred_element_type=F32)
        new_real = total[:windows] + total[windows:2 * windows]
        new_imag = total[2 * windows:3 * windows] + total[3 * windows:]
        power = jnp.sum(new_real * new_real + new_imag * new_imag, axis=1, keepdims=True) * (1.0 / 128)
        scale = lax.rsqrt(power + 1e-05)
        vec_real, vec_imag = new_real * scale, new_imag * scale
    return vec_real, vec_imag


def kernel(
    n, slc_ref, usable_ref, coherence, linked, plane, split1, split2, send, recv, turn, note, notes,
    send_sem, recv_sem, note_send, note_recv,
):
    looks, dates = slc_ref.shape[1], slc_ref.shape[2]
    me = lax.axis_index("date")
    barrier = pltpu.get_barrier_semaphore()
    order = []
    for k in range(n // 2, 0, -1):
        order += [k] if 2 * k == n else [k, n - k]
    for k in order:
        pl.semaphore_signal(barrier, inc=1, device_id={"date": lax.rem(me + k, n)}, device_id_type=MESH)

    pack(slc_ref, usable_ref, plane, split1, split2, send, looks, dates, n)
    pl.semaphore_wait(barrier, n - 1)

    def sample_copy(k):
        to = lax.rem(me + k, n)
        return pltpu.make_async_remote_copy(
            src_ref=send.at[to], dst_ref=recv.at[:, me], send_sem=send_sem.at[k], recv_sem=recv_sem.at[k],
            device_id={"date": to}, device_id_type=MESH,
        )

    for k in order:
        sample_copy(k).start()
    recv[:, me] = send[me]
    for k in order:
        source = lax.rem(me + n - k, n)
        pltpu.make_async_remote_copy(
            src_ref=send.at[source], dst_ref=recv.at[:, source], send_sem=send_sem.at[k], recv_sem=recv_sem.at[k],
            device_id={"date": source}, device_id_type=MESH,
        ).wait_recv()

    for i in range(T1):
        gram(recv, coherence, i, looks)
    vec_real, vec_imag = link(coherence, T1)

    rows = jnp.concatenate([vec_real] + [vec_imag] * 4 + [vec_real] * 3, axis=0)
    turn[...] = rows.T
    lane = lane_iota((2 * n, 128))
    message = jnp.zeros((2 * n, 128), F32)
    for q in range(4):
        message = jnp.where((8 - lane // 16) % 4 == q, turn[pl.ds(q, 2 * n, stride=4), :], message)
    for d in range(n):
        note[d] = message[2 * d:2 * d + 2]

    def note_copy(k):
        to = lax.rem(me + k, n)
        return pltpu.make_async_remote_copy(
            src_ref=note.at[to], dst_ref=notes.at[me], send_sem=note_send.at[k], recv_sem=note_recv.at[k],
            device_id={"date": to}, device_id_type=MESH,
        )

    for k in order:
        note_copy(k).start()
    notes[me] = note[me]
    for k in order:
        source = lax.rem(me + n - k, n)
        pltpu.make_async_remote_copy(
            src_ref=note.at[source], dst_ref=notes.at[source], send_sem=note_send.at[k], recv_sem=note_recv.at[k],
            device_id={"date": source}, device_id_type=MESH,
        ).wait_recv()

    lane = lane_iota((8, 128))
    for h in range(2):
        for half in range(2):
            tile = jnp.zeros((8, 128), F32)
            came = jnp.concatenate([notes[half * 8 + s, h:h + 1, :] for s in range(8)], axis=0)
            came = pltpu.roll(came, 0, 1, stride=16, stride_axis=0)
            for s in range(8):
                source = jnp.broadcast_to(came[s:s + 1], (8, 128))
                moved = pltpu.roll(source, 0, 1, stride=16, stride_axis=0)
                tile = jnp.where(lane // 16 == s, moved, tile)
            for c in range(2):
                linked[c, 4 * h:4 * h + 4, half * 128:half * 128 + 128] = tile[4 * c:4 * c + 4]
    for k in order:
        sample_copy(k).wait_send()
        note_copy(k).wait_send()


def solution(mesh):
    n = mesh.shape["date"]

    def step(slc, usable):
        dates, windows = slc.shape[2], slc.shape[3]
        rows = 2 * slc.shape[1] * dates
        per_device = windows // n
        vmem = pl.BlockSpec(memory_space=pltpu.VMEM)
        return pl.pallas_call(
            functools.partial(kernel, n),
            out_shape=(
                jax.ShapeDtypeStruct((2, 1, 1, per_device, n * dates, n * dates), BF16),
                jax.ShapeDtypeStruct((2, dates, windows), F32),
            ),
            in_specs=[vmem, vmem],
            out_specs=(vmem, vmem),
            scratch_shapes=[
                pltpu.VMEM((windows // 128, rows, 128), F32),
                pltpu.VMEM((windows * dates, 128), F32),
                pltpu.VMEM((windows * dates // 2, 128), F32),
                pltpu.VMEM((n, TILES, dates, 128), BF16),
                pltpu.VMEM((TILES, n, dates, 128), BF16),
                pltpu.VMEM((128, 128), F32),
                pltpu.VMEM((n, 2, 128), F32),
                pltpu.VMEM((n, 2, 128), F32),
                pltpu.SemaphoreType.DMA((n,)),
                pltpu.SemaphoreType.DMA((n,)),
                pltpu.SemaphoreType.DMA((n,)),
                pltpu.SemaphoreType.DMA((n,)),
            ],
            compiler_params=pltpu.CompilerParams(collective_id=0, has_side_effects=True),
        )(slc, usable)

    return jax.shard_map(
        step,
        mesh=mesh,
        in_specs=(
            P(None, None, "date", ("slab", "tile", "sub")),
            P(None, "date", ("slab", "tile", "sub")),
        ),
        out_specs=(
            P(None, ("slab", "tile", "sub"), "date", None, None, None),
            P(None, "date", ("slab", "tile", "sub")),
        ),
        check_vma=False,
    )
```

time: 140 us -> 100 us (0.71)
  Pallas kernels: 0 us -> 96.6 us
  blocking collectives: 89.3 us -> 0 us
  matrix products: 16.5 us -> 0 us
  starting transfers between devices: 12.7 us -> 0 us
  waiting for transfers between devices: 10.1 us -> 0 us
  local copies, waits for them, and re-layouts: 6.45 us -> 2.92 us
  other arithmetic: 3.38 us -> 0 us
    pallas_call x0 -> x1, Pallas kernels: none -> 96.6 us  [step(): pl.pallas_call(functools.partial(kernel, n), out_shape=(jax.ShapeDtypeStr...]
    all_to_all x1 -> x0, blocking collectives: 89.3 us -> none  [local(): lax.all_to_all(split_view, 'date', split_axis=3, concat_axis=2, tiled=True)]
    dot_general x20 -> x0, matrix products: 16.5 us -> none  [the longest x4 3.7 us: complex_apply(): jnp.einsum('wab,bw->aw', matrix[1], vec_real, precision=lax.Precision.HIG...]
    all_to_all x1 -> x0, starting transfers between devices: 12.7 us -> none  [local(): lax.all_to_all(jnp.stack([vec_real, vec_imag]), 'date', split_axis=1, con...]
    all_to_all x1 -> x0, waiting for transfers between devices: 10.1 us -> none  [local(): lax.all_to_all(jnp.stack([vec_real, vec_imag]), 'date', split_axis=1, con...]
    unnamed x5 -> x4, local copies, waits for them, and re-layouts: 2.95 us -> 2.92 us
  transfers between devices with their start and end apart: 1 -> 0, of which waited for: 1 -> 0; matrix products, arithmetic and copies ran while one was open for 1% -> 0% of each run, Pallas kernels for 0% -> 0%
where the time goes in v1:
time: 100 us
  Pallas kernels  96.6 us (97%)
  local copies, waits for them, and re-layouts  2.92 us (3%)
    pallas_call x1, Pallas kernels, step(): pl.pallas_call(functools.partial(kernel, n), out_shape=(jax.ShapeDtypeStr...  96.6 us
    unnamed x4, local copies, waits for them, and re-layouts  2.92 us

profile of v1, /device:TPU:65, one launch (start us, length us, event | category | flops | bytes accessed | tf_op | source)
XLA Modules:
  0.0 100.1 jit_solution(10420759085876890933)
XLA Ops:
  0.6 96.6 %shard_map.41 = (bf16[2,1,1,16,128,128]{5,4,3,2,1,0:T(8,128)(2,1)}, f32[2,8,256]{2,1,0:T(8,128)}) custom-call(bf16[2,100,8,256]{3,2,1,0:T(8,128)(2,1)} %slc_ref.1, s32[100,8,256]{2,1,0:T(8,128)} %usable_ref.1), custom_call_target="tpu_custom_call" | custom-call | tf_op jit(solution)/shard_map/pallas_call | solution.py:215
  97.2 0.0 copy-start
  97.2 2.3 %copy.6 = bf16[2,1,1,16,128,128]{5,4,3,2,1,0:T(8,128)(2,1)} copy(bf16[2,1,1,16,128,128]{5,4,3,2,1,0:T(8,128)(2,1)} %get-tuple-element.4) | data formatting | bytes 2097152
  99.5 0.0 copy-done
  99.5 0.6 copy.7
Async XLA Ops:
  97.2 2.3 %copy-start = (f32[2,8,256]{2,1,0:T(8,128)S(1)}, f32[2,8,256]{2,1,0:T(8,128)}, u32[]{:S(2)}) copy-start(f32[2,8,256]{2,1,0:T(8,128)} %get-tuple-element.5) | copy-start | bytes 49156

commit v2 on v1

v2 whole, which is shorter than its diff:
```python
import functools

import jax
import jax.numpy as jnp
from jax import lax
from jax.experimental import pallas as pl
from jax.experimental.pallas import tpu as pltpu
from jax.sharding import PartitionSpec as P

ITERS = 4
MESH = pl.DeviceIdType.MESH
F32, BF16 = jnp.float32, jnp.bfloat16
WINDOWS = 16
LOADS = 5
CHUNKS = ((0, 13), (13, 12))
TILES = 25
REST = 12


def places(i):
    chunk, spot = divmod(i % 8, 4)
    return CHUNKS[chunk][0] + 4 * (i // 8) + spot, CHUNKS[chunk][0] + 8 + spot


def lane_iota(shape):
    return lax.broadcasted_iota(jnp.int32, shape, len(shape) - 1)


def pack(slc_ref, usable_ref, plane, split1, split2, send, loads, looks, dates, blocks):
    rows = looks * dates
    step = looks // LOADS

    def mask_step(l, carry):
        use = usable_ref[l].astype(F32)
        for c in range(2):
            masked = slc_ref[c, l].astype(F32) * use
            at = pl.ds(pl.multiple_of(c * rows + l * dates, 8), dates)
            for half in range(2):
                plane[half, at, :] = masked[:, half * 128:half * 128 + 128]
        return carry

    with jax.named_scope("mask"):
        for piece, copies in enumerate(loads):
            for copy in copies:
                copy.wait()
            lax.fori_loop(piece * step, piece * step + step, mask_step, 0, unroll=4)

    bit = (lane_iota((8, 8, 128)) // 8) % 2 == 1
    groups = [(c, r) for c in range(2) for r in range(4)]
    for half in range(2):

        def group(a, c, look, count):
            return plane[half, pl.ds(c * rows + look * dates + a, count, stride=dates), :]

        def date_step(a, carry):
            first = jnp.concatenate([group(a, c, 0, 64) for c in range(2)], axis=0)
            split1[pl.ds(half * 1024 + a, 128, stride=8), :] = first.T
            parts = []
            for c in range(2):
                for u in range(4):
                    rest = group(a, c, 64 + 8 * u, 8)
                    parts += [rest, rest]
            second = jnp.concatenate(parts, axis=0).T.reshape(8, 2, 8, 128)
            pairs = jnp.where(bit, second[:, 0], second[:, 1]).reshape(64, 128)
            split2[pl.ds(half * 512 + a, 64, stride=8), :] = pairs
            return carry

        lax.fori_loop(0, dates, date_step, 0, unroll=4)

        left = [plane[half, c * rows + (96 + r) * dates:c * rows + (97 + r) * dates, :] for c, r in groups]
        for b in range(8):
            tile = jnp.zeros((8, 128), F32)
            for g, part in enumerate(left):
                shift = (16 * (g - b)) % 128
                moved = pltpu.roll(part, shift, 1) if shift else part
                tile = jnp.where(lane_iota((8, 128)) // 16 == g, moved, tile)
            send[half * 8 + b, REST] = tile.astype(BF16)

    def out_step(b, carry):
        one = split1[pl.ds(pl.multiple_of(b * 128, 128), 128), :].reshape(16, 8, 128).astype(BF16)
        two = split2[pl.ds(pl.multiple_of(b * 64, 64), 64), :].reshape(8, 8, 128).astype(BF16)
        for chunk, (base, _) in enumerate(CHUNKS):
            send[b, base:base + 4] = one[4 * chunk:4 * chunk + 4]
            send[b, base + 4:base + 8] = one[8 + 4 * chunk:12 + 4 * chunk]
            send[b, base + 8:base + 12] = two[4 * chunk:4 * chunk + 4]
        return carry

    with jax.named_scope("cast"):
        lax.fori_loop(0, blocks, out_step, 0)


def gram(recv, coherence, i, looks):
    lane = lane_iota((128, 128))
    own, shared = places(i)
    one = recv[own].astype(F32).reshape(128, 128)
    pair = recv[shared].astype(F32).reshape(128, 128)
    rest = recv[REST].astype(F32).reshape(128, 128)
    in_pair = ((lane // 8) % 2 == 1) == (i < 8)
    two = jnp.where(in_pair, pair, jnp.where(lane % 16 == i, rest, 0.0))
    sign = jnp.where(lane < 64, 1.0, -1.0)
    plain = jnp.concatenate([one, two], axis=1).astype(BF16)
    turned = jnp.concatenate([pltpu.roll(one, 64, 1) * sign, pltpu.roll(two, 64, 1) * sign], axis=1).astype(BF16)
    both = jnp.concatenate([plain, turned], axis=0)
    cross = lax.dot_general(both, plain, (((1,), (1,)), ((), ())), preferred_element_type=F32)
    real, imag = cross[:128], cross[128:]
    eye = lax.broadcasted_iota(jnp.int32, (128, 128), 0) == lane
    diagonal = jnp.where(eye, real, 0.0)
    column = lax.rsqrt(jnp.sum(diagonal, axis=1, keepdims=True) * (1.0 / looks) + 1e-05)
    row = lax.rsqrt(jnp.sum(diagonal, axis=0, keepdims=True) * (1.0 / looks) + 1e-05)
    factor = column * row * (1.0 / looks)
    coherence[0, 0, 0, i] = (real * factor).astype(BF16)
    coherence[1, 0, 0, i] = (imag * factor).astype(BF16)


def link(coherence, windows):
    row = lax.broadcasted_iota(jnp.int32, (4 * windows, 256), 0) % windows
    real, imag = jnp.ones((windows, 128), F32), jnp.zeros((windows, 128), F32)
    scale = None
    for step in range(ITERS):
        high_real, high_imag = real.astype(BF16).astype(F32), imag.astype(BF16).astype(F32)
        low_real, low_imag = real - high_real, imag - high_imag
        lhs = jnp.concatenate(
            [
                jnp.concatenate([high_real, high_imag], axis=1),
                jnp.concatenate([low_real, low_imag], axis=1),
                jnp.concatenate([high_imag, -high_real], axis=1),
                jnp.concatenate([low_imag, -low_real], axis=1),
            ],
            axis=0,
        )
        total = jnp.zeros((4 * windows, 128), F32)
        for w in range(windows):
            stacked = jnp.concatenate([coherence[0, 0, 0, w], coherence[1, 0, 0, w]], axis=0)
            total += jnp.dot(jnp.where(row == w, lhs, 0.0).astype(BF16), stacked, preferred_element_type=F32)
        real = total[:windows] + total[windows:2 * windows]
        imag = total[2 * windows:3 * windows] + total[3 * windows:]
        if scale is not None:
            real, imag = real * scale, imag * scale
        scale = lax.rsqrt(jnp.sum(real * real + imag * imag, axis=1, keepdims=True) * (1.0 / 128) + 1e-05)
    return real * scale, imag * scale


def kernel(
    n, slc_hbm, usable_hbm, coherence, notes, slc_ref, usable_ref, plane, split1, split2, send, recv, turn, note,
    load_sem, send_sem, recv_sem, note_send, note_recv,
):
    looks, dates = slc_ref.shape[1], slc_ref.shape[2]
    me = lax.axis_index("date")
    barrier = pltpu.get_barrier_semaphore()
    order = []
    for k in range(n // 2, 0, -1):
        order += [k] if 2 * k == n else [k, n - k]
    loads = []
    for piece in range(LOADS):
        part = pl.ds(piece * (looks // LOADS), looks // LOADS)
        loads.append([
            pltpu.make_async_copy(slc_hbm.at[0, part], slc_ref.at[0, part], load_sem.at[piece, 0]),
            pltpu.make_async_copy(slc_hbm.at[1, part], slc_ref.at[1, part], load_sem.at[piece, 1]),
            pltpu.make_async_copy(usable_hbm.at[part], usable_ref.at[part], load_sem.at[piece, 2]),
        ])
        for copy in loads[-1]:
            copy.start()
    for k in order:
        pl.semaphore_signal(barrier, inc=1, device_id={"date": lax.rem(me + k, n)}, device_id_type=MESH)

    pack(slc_ref, usable_ref, plane, split1, split2, send, loads, looks, dates, n)
    with jax.named_scope("barrier"):
        pl.semaphore_wait(barrier, n - 1)

    def sample_copy(k, chunk, to, slot):
        tiles = pl.ds(*CHUNKS[chunk])
        return pltpu.make_async_remote_copy(
            src_ref=send.at[to, tiles], dst_ref=recv.at[tiles, slot], send_sem=send_sem.at[0], recv_sem=recv_sem.at[chunk, k],
            device_id={"date": to}, device_id_type=MESH,
        )

    with jax.named_scope("start"):
        for chunk in range(2):
            for k in order:
                sample_copy(k, chunk, lax.rem(me + k, n), me).start()
        recv[:, me] = send[me]
    for chunk in range(2):
        with jax.named_scope("receive"):
            for k in order:
                source = lax.rem(me + n - k, n)
                sample_copy(k, chunk, source, source).wait_recv()
        with jax.named_scope("gram"):
            for i in range(WINDOWS):
                if (i % 8) // 4 == chunk:
                    gram(recv, coherence, i, looks)
    with jax.named_scope("link"):
        vec_real, vec_imag = link(coherence, WINDOWS)

    with jax.named_scope("note"):
        rows = jnp.concatenate([vec_real] + [vec_imag] * 4 + [vec_real] * 3, axis=0)
        turn[...] = rows.T
        lane = lane_iota((2 * n, 128))
        message = jnp.zeros((2 * n, 128), F32)
        for q in range(4):
            message = jnp.where((8 - lane // 16) % 4 == q, turn[pl.ds(q, 2 * n, stride=4), :], message)
        for d in range(n):
            note[d] = message[2 * d:2 * d + 2]

    def note_copy(k):
        to = lax.rem(me + k, n)
        return pltpu.make_async_remote_copy(
            src_ref=note.at[to], dst_ref=notes.at[me], send_sem=note_send.at[0], recv_sem=note_recv.at[k],
            device_id={"date": to}, device_id_type=MESH,
        )

    with jax.named_scope("notes"):
        for k in order:
            note_copy(k).start()
        notes[me] = note[me]
        pltpu.make_async_copy(send.at[0:n - 1], send.at[0:n - 1], send_sem.at[0]).wait()
        for k in order:
            source = lax.rem(me + n - k, n)
            pltpu.make_async_remote_copy(
                src_ref=note.at[source], dst_ref=notes.at[source], send_sem=note_send.at[0], recv_sem=note_recv.at[k],
                device_id={"date": source}, device_id_type=MESH,
            ).wait_recv()

    pltpu.make_async_copy(note.at[0:n - 1], note.at[0:n - 1], note_send.at[0]).wait()


def store(coherence, notes, coherence_out, linked_out, linked, sem):
    copies = [pltpu.make_async_copy(coherence.at[:, :, :, i], coherence_out.at[:, :, :, i], sem.at[i]) for i in range(WINDOWS)]
    for copy in copies:
        copy.start()
    lane = lane_iota((8, 128))
    for h in range(2):
        for half in range(2):
            tile = jnp.zeros((8, 128), F32)
            came = jnp.concatenate([notes[half * 8 + s, h:h + 1, :] for s in range(8)], axis=0)
            came = pltpu.roll(came, 0, 1, stride=16, stride_axis=0)
            for s in range(8):
                source = jnp.broadcast_to(came[s:s + 1], (8, 128))
                moved = pltpu.roll(source, 0, 1, stride=16, stride_axis=0)
                tile = jnp.where(lane // 16 == s, moved, tile)
            for c in range(2):
                linked[c, 4 * h:4 * h + 4, half * 128:half * 128 + 128] = tile[4 * c:4 * c + 4]
    copies.append(pltpu.make_async_copy(linked, linked_out, sem.at[WINDOWS]))
    copies[-1].start()
    for copy in copies:
        copy.wait()


def solution(mesh):
    n = mesh.shape["date"]

    def step(slc, usable):
        dates, windows = slc.shape[2], slc.shape[3]
        rows = 2 * slc.shape[1] * dates
        per_device = windows // n
        vmem, hbm = pl.BlockSpec(memory_space=pltpu.VMEM), pl.BlockSpec(memory_space=pl.ANY)
        coherence_shape, linked_shape = (2, 1, 1, per_device, n * dates, n * dates), (2, dates, windows)
        coherence, notes = pl.pallas_call(
            functools.partial(kernel, n),
            out_shape=(pltpu.VMEM(coherence_shape, BF16), pltpu.VMEM((n, 2, 128), F32)),
            in_specs=[hbm, hbm],
            out_specs=(vmem, vmem),
            scratch_shapes=[
                pltpu.VMEM(slc.shape, BF16),
                pltpu.VMEM(usable.shape, jnp.int32),
                pltpu.VMEM((windows // 128, rows, 128), F32),
                pltpu.VMEM((windows * dates, 128), F32),
                pltpu.VMEM((windows * dates // 2, 128), F32),
                pltpu.VMEM((n, TILES, dates, 128), BF16),
                pltpu.VMEM((TILES, n, dates, 128), BF16),
                pltpu.VMEM((128, 128), F32),
                pltpu.VMEM((n, 2, 128), F32),
                pltpu.SemaphoreType.DMA((LOADS, 3)),
                pltpu.SemaphoreType.DMA((1,)),
                pltpu.SemaphoreType.DMA((2, n)),
                pltpu.SemaphoreType.DMA((1,)),
                pltpu.SemaphoreType.DMA((n,)),
            ],
            compiler_params=pltpu.CompilerParams(collective_id=0, has_side_effects=True),
        )(slc, usable)
        return pl.pallas_call(
            store,
            out_shape=(jax.ShapeDtypeStruct(coherence_shape, BF16), jax.ShapeDtypeStruct(linked_shape, F32)),
            in_specs=[vmem, vmem],
            out_specs=(hbm, hbm),
            scratch_shapes=[pltpu.VMEM(linked_shape, F32), pltpu.SemaphoreType.DMA((WINDOWS + 1,))],
        )(pltpu.with_memory_space_constraint(coherence, pltpu.VMEM), pltpu.with_memory_space_constraint(notes, pltpu.VMEM))

    return jax.shard_map(
        step,
        mesh=mesh,
        in_specs=(
            P(None, None, "date", ("slab", "tile", "sub")),
            P(None, "date", ("slab", "tile", "sub")),
        ),
        out_specs=(
            P(None, ("slab", "tile", "sub"), "date", None, None, None),
            P(None, "date", ("slab", "tile", "sub")),
        ),
        check_vma=False,
    )
```

time: 100 us -> 95 us (0.950)
  local copies, waits for them, and re-layouts: 2.92 us -> 0 us
  Pallas kernels: 96.6 us -> 94.2 us
    unnamed x4 -> x0, local copies, waits for them, and re-layouts: 2.92 us -> none
    pallas_call x1 -> x2, Pallas kernels: 96.6 us -> 94.2 us  [the longest x1 93.1 us: step(): pl.pallas_call(functools.partial(kernel, n), out_shape=(pltpu.VMEM(cohere...]
where the time goes in v2:
time: 95 us; the launch traced here: 94.9 us
  Pallas kernels  94.2 us (99%)
    pallas_call x1, Pallas kernels, step(): pl.pallas_call(functools.partial(kernel, n), out_shape=(pltpu.VMEM(cohere...  93.1 us

profile of v2, /device:TPU:65, one launch (start us, length us, event | category | flops | bytes accessed | tf_op | source)
XLA Modules:
  0.0 94.9 jit_solution(11144559853700976041)
XLA Ops:
  0.6 93.1 %shard_map.41 = (bf16[2,1,1,16,128,128]{5,4,3,2,1,0:T(8,128)(2,1)S(1)}, f32[16,2,128]{2,1,0:T(2,128)S(1)}) custom-call(bf16[2,100,8,256]{3,2,1,0:T(8,128)(2,1)} %slc_hbm.1, s32[100,8,256]{2,1,0:T(8,128)} %usable_hbm.1), custom_call_target="tpu_custom_call" | custom-call | tf_op jit(solution)/shard_map/pallas_call | solution.py:257
  93.8 1.1 %shard_map.42 = (bf16[2,1,1,16,128,128]{5,4,3,2,1,0:T(8,128)(2,1)}, f32[2,8,256]{2,1,0:T(8,128)}) custom-call(bf16[2,1,1,16,128,128]{5,4,3,2,1,0:T(8,128)(2,1)S(1)} %get-tuple-element.4.coherence, f32[16,2,128]{2,1,0:T(2,128)S(1)} %get-tuple-element.5.notes), custom_call_target="tpu_custom_call" | custom-call | tf_op jit(solution)/shard_map/pallas_call | solution.py:280

commit v3 on v2

--- a/solution.py
+++ b/solution.py
@@ -26,7 +26,7 @@
     return lax.broadcasted_iota(jnp.int32, shape, len(shape) - 1)
 
 
-def pack(slc_ref, usable_ref, plane, split1, split2, send, loads, looks, dates, blocks):
+def pack(slc_ref, usable_ref, plane, split1, split2, send, loads, between, looks, dates, blocks):
     rows = looks * dates
     step = looks // LOADS
 
@@ -44,6 +44,8 @@
             for copy in copies:
                 copy.wait()
             lax.fori_loop(piece * step, piece * step + step, mask_step, 0, unroll=4)
+    with jax.named_scope("greet"):
+        between()
 
     bit = (lane_iota((8, 8, 128)) // 8) % 2 == 1
     groups = [(c, r) for c in range(2) for r in range(4)]
@@ -142,7 +144,7 @@
 
 def kernel(
     n, slc_hbm, usable_hbm, coherence, notes, slc_ref, usable_ref, plane, split1, split2, send, recv, turn, note,
-    load_sem, send_sem, recv_sem, note_send, note_recv,
+    load_sem, send_sem, recv_sem, note_send, note_recv, lower_sem, known_sem,
 ):
     looks, dates = slc_ref.shape[1], slc_ref.shape[2]
     me = lax.axis_index("date")
@@ -160,12 +162,29 @@
         ])
         for copy in loads[-1]:
             copy.start()
-    for k in order:
-        pl.semaphore_signal(barrier, inc=1, device_id={"date": lax.rem(me + k, n)}, device_id_type=MESH)
-
-    pack(slc_ref, usable_ref, plane, split1, split2, send, loads, looks, dates, n)
-    with jax.named_scope("barrier"):
-        pl.semaphore_wait(barrier, n - 1)
+    rank = lax.rem(me + n - 1, n)
+    after, before = lax.rem(me + 1, n), lax.rem(me + n - 1, n)
+    pl.semaphore_signal(barrier, inc=1, device_id={"date": before}, device_id_type=MESH)
+
+    def greet():
+        pl.semaphore_wait(barrier, 1)
+
+        @pl.when(rank > 0)
+        def _():
+            pl.semaphore_wait(lower_sem, 1)
+
+        for k in range(2, n):
+
+            @pl.when(rank >= k)
+            def _():
+                pl.semaphore_signal(known_sem.at[k], inc=1, device_id={"date": lax.rem(me + n - k, n)}, device_id_type=MESH)
+
+        @pl.when(rank < n - 1)
+        def _():
+            pl.semaphore_signal(lower_sem, inc=1, device_id={"date": after}, device_id_type=MESH)
+
+    pack(slc_ref, usable_ref, plane, split1, split2, send, loads, lambda: pl.when(rank < n - 1)(greet), looks, dates, n)
+    pl.when(rank == n - 1)(greet)
 
     def sample_copy(k, chunk, to, slot):
         tiles = pl.ds(*CHUNKS[chunk])
@@ -175,10 +194,23 @@
         )
 
     with jax.named_scope("start"):
-        for chunk in range(2):
-            for k in order:
-                sample_copy(k, chunk, lax.rem(me + k, n), me).start()
+        for k in order:
+
+            @pl.when(rank + k >= n)
+            def _():
+                for chunk in range(2):
+                    sample_copy(k, chunk, lax.rem(me + k, n), me).start()
+
         recv[:, me] = send[me]
+        for k in range(1, n):
+
+            @pl.when(rank + k < n)
+            def _():
+                if k > 1:
+                    pl.semaphore_wait(known_sem.at[k], 1)
+                for chunk in range(2):
+                    sample_copy(k, chunk, lax.rem(me + k, n), me).start()
+
     for chunk in range(2):
         with jax.named_scope("receive"):
             for k in order:
@@ -274,6 +306,8 @@
                 pltpu.SemaphoreType.DMA((2, n)),
                 pltpu.SemaphoreType.DMA((1,)),
                 pltpu.SemaphoreType.DMA((n,)),
+                pltpu.SemaphoreType.REGULAR,
+                pltpu.SemaphoreType.REGULAR((n,)),
             ],
             compiler_params=pltpu.CompilerParams(collective_id=0, has_side_effects=True),
         )(slc, usable)

time: 95 us -> 87.1 us (0.917)
  Pallas kernels: 94.2 us -> 85.4 us
    pallas_call x1, Pallas kernels: 93.1 us -> 84.3 us  [step(): pl.pallas_call(functools.partial(kernel, n), out_shape=(pltpu.VMEM(cohere...]
where the time goes in v3:
time: 87.1 us; the launch traced here: 86 us
  Pallas kernels  85.4 us (98%)
    pallas_call x1, Pallas kernels, step(): pl.pallas_call(functools.partial(kernel, n), out_shape=(pltpu.VMEM(cohere...  84.3 us

profile of v3, /device:TPU:65, one launch (start us, length us, event | category | flops | bytes accessed | tf_op | source)
XLA Modules:
  0.0 86.0 jit_solution(2995032678885108799)
XLA Ops:
  0.6 84.3 %shard_map.41 = (bf16[2,1,1,16,128,128]{5,4,3,2,1,0:T(8,128)(2,1)S(1)}, f32[16,2,128]{2,1,0:T(2,128)S(1)}) custom-call(bf16[2,100,8,256]{3,2,1,0:T(8,128)(2,1)} %slc_hbm.1, s32[100,8,256]{2,1,0:T(8,128)} %usable_hbm.1), custom_call_target="tpu_custom_call" | custom-call | tf_op jit(solution)/shard_map/pallas_call | solution.py:289
  84.9 1.1 %shard_map.42 = (bf16[2,1,1,16,128,128]{5,4,3,2,1,0:T(8,128)(2,1)}, f32[2,8,256]{2,1,0:T(8,128)}) custom-call(bf16[2,1,1,16,128,128]{5,4,3,2,1,0:T(8,128)(2,1)S(1)} %get-tuple-element.4.coherence, f32[16,2,128]{2,1,0:T(2,128)S(1)} %get-tuple-element.5.notes), custom_call_target="tpu_custom_call" | custom-call | tf_op jit(solution)/shard_map/pallas_call | solution.py:314

commit v4 on v2

--- a/solution.py
+++ b/solution.py
@@ -11,6 +11,7 @@
 MESH = pl.DeviceIdType.MESH
 F32, BF16 = jnp.float32, jnp.bfloat16
 WINDOWS = 16
+LATE = 3
 LOADS = 5
 CHUNKS = ((0, 13), (13, 12))
 TILES = 25
@@ -26,7 +27,7 @@
     return lax.broadcasted_iota(jnp.int32, shape, len(shape) - 1)
 
 
-def pack(slc_ref, usable_ref, plane, split1, split2, send, loads, looks, dates, blocks):
+def pack(slc_ref, usable_ref, plane, split1, split2, send, loads, between, looks, dates, blocks):
     rows = looks * dates
     step = looks // LOADS
 
@@ -44,6 +45,7 @@
             for copy in copies:
                 copy.wait()
             lax.fori_loop(piece * step, piece * step + step, mask_step, 0, unroll=4)
+    between()
 
     bit = (lane_iota((8, 8, 128)) // 8) % 2 == 1
     groups = [(c, r) for c in range(2) for r in range(4)]
@@ -112,7 +114,8 @@
     coherence[1, 0, 0, i] = (imag * factor).astype(BF16)
 
 
-def link(coherence, windows):
+def link(coherence, members):
+    windows = len(members)
     row = lax.broadcasted_iota(jnp.int32, (4 * windows, 256), 0) % windows
     real, imag = jnp.ones((windows, 128), F32), jnp.zeros((windows, 128), F32)
     scale = None
@@ -129,8 +132,8 @@
             axis=0,
         )
         total = jnp.zeros((4 * windows, 128), F32)
-        for w in range(windows):
-            stacked = jnp.concatenate([coherence[0, 0, 0, w], coherence[1, 0, 0, w]], axis=0)
+        for w, i in enumerate(members):
+            stacked = jnp.concatenate([coherence[0, 0, 0, i], coherence[1, 0, 0, i]], axis=0)
             total += jnp.dot(jnp.where(row == w, lhs, 0.0).astype(BF16), stacked, preferred_element_type=F32)
         real = total[:windows] + total[windows:2 * windows]
         imag = total[2 * windows:3 * windows] + total[3 * windows:]
@@ -142,7 +145,7 @@
 
 def kernel(
     n, slc_hbm, usable_hbm, coherence, notes, slc_ref, usable_ref, plane, split1, split2, send, recv, turn, note,
-    load_sem, send_sem, recv_sem, note_send, note_recv,
+    load_sem, send_sem, recv_sem, note_send, note_recv, known_sem,
 ):
     looks, dates = slc_ref.shape[1], slc_ref.shape[2]
     me = lax.axis_index("date")
@@ -154,42 +157,108 @@
     for piece in range(LOADS):
         part = pl.ds(piece * (looks // LOADS), looks // LOADS)
         loads.append([
-            pltpu.make_async_copy(slc_hbm.at[0, part], slc_ref.at[0, part], load_sem.at[piece, 0]),
-            pltpu.make_async_copy(slc_hbm.at[1, part], slc_ref.at[1, part], load_sem.at[piece, 1]),
-            pltpu.make_async_copy(usable_hbm.at[part], usable_ref.at[part], load_sem.at[piece, 2]),
+            pltpu.make_async_copy(slc_hbm.at[:, part], slc_ref.at[:, part], load_sem.at[piece, 0]),
+            pltpu.make_async_copy(usable_hbm.at[part], usable_ref.at[part], load_sem.at[piece, 1]),
         ])
         for copy in loads[-1]:
             copy.start()
-    for k in order:
-        pl.semaphore_signal(barrier, inc=1, device_id={"date": lax.rem(me + k, n)}, device_id_type=MESH)
-
-    pack(slc_ref, usable_ref, plane, split1, split2, send, loads, looks, dates, n)
-    with jax.named_scope("barrier"):
-        pl.semaphore_wait(barrier, n - 1)
-
-    def sample_copy(k, chunk, to, slot):
+
+    first = me == 0
+
+    def rank_of(z):
+        if isinstance(z, int):
+            return n - 2 if z in (0, n - 1) else z - 1
+        return jnp.where((z == 0) | (z == n - 1), n - 2, z - 1)
+
+    rank = rank_of(me)
+
+    def enter():
+        @pl.when(rank > 0)
+        def _():
+            pl.semaphore_wait(barrier, 1)
+
+        @pl.when(rank < n - 2)
+        def _():
+            pl.semaphore_signal(barrier, inc=1, device_id={"date": me + 1}, device_id_type=MESH)
+
+        @pl.when(me == n - 2)
+        def _():
+            pl.semaphore_signal(barrier, inc=1, device_id={"date": 0}, device_id_type=MESH)
+
+        for k in order:
+            to = lax.rem(me + k, n)
+
+            @pl.when(rank_of(to) < rank)
+            def _():
+                pl.semaphore_signal(known_sem.at[me], inc=1, device_id={"date": to}, device_id_type=MESH)
+
+    pl.when(me > 0)(enter)
+    pack(slc_ref, usable_ref, plane, split1, split2, send, loads, lambda: pl.when(first)(enter), looks, dates, n)
+
+    def sample_copy(chunk, to, source):
         tiles = pl.ds(*CHUNKS[chunk])
         return pltpu.make_async_remote_copy(
-            src_ref=send.at[to, tiles], dst_ref=recv.at[tiles, slot], send_sem=send_sem.at[0], recv_sem=recv_sem.at[chunk, k],
+            src_ref=send.at[to, tiles], dst_ref=recv.at[tiles, source], send_sem=send_sem.at[0], recv_sem=recv_sem.at[chunk, source],
             device_id={"date": to}, device_id_type=MESH,
         )
 
+    def send_lower(chunk):
+        for k in order:
+            to = lax.rem(me + k, n)
+
+            @pl.when(rank_of(to) < rank)
+            def _():
+                sample_copy(chunk, to, me).start()
+
+    late = n - LATE
+    entry = [*range(1, n - 1), 0, n - 1]
     with jax.named_scope("start"):
-        for chunk in range(2):
-            for k in order:
-                sample_copy(k, chunk, lax.rem(me + k, n), me).start()
+        send_lower(0)
+        pl.when(rank < late)(lambda: send_lower(1))
         recv[:, me] = send[me]
+        for place, z in enumerate(entry):
+
+            @pl.when(rank < rank_of(z))
+            def _():
+                pl.semaphore_wait(known_sem.at[z], 1)
+                for chunk in range(2 if place < late else 1):
+                    sample_copy(chunk, z, me).start()
+
+        @pl.when(me == n - 2)
+        def _():
+            pl.semaphore_signal(known_sem.at[0], inc=1, device_id={"date": n - 1}, device_id_type=MESH)
+            pl.semaphore_signal(known_sem.at[n - 1], inc=1, device_id={"date": 0}, device_id_type=MESH)
+
+        pl.when(rank >= late)(lambda: send_lower(1))
+        for z in entry[late:]:
+
+            @pl.when(rank < rank_of(z))
+            def _():
+                sample_copy(1, z, me).start()
+
+        for one, other in ((0, n - 1), (n - 1, 0)):
+
+            @pl.when(me == one)
+            def _():
+                pl.semaphore_wait(known_sem.at[other], 1)
+                for chunk in range(2):
+                    sample_copy(chunk, other, me).start()
+
+    linked = []
     for chunk in range(2):
         with jax.named_scope("receive"):
             for k in order:
                 source = lax.rem(me + n - k, n)
-                sample_copy(k, chunk, source, source).wait_recv()
+                sample_copy(chunk, source, source).wait_recv()
+        members = [i for i in range(WINDOWS) if (i % 8) // 4 == chunk]
         with jax.named_scope("gram"):
-            for i in range(WINDOWS):
-                if (i % 8) // 4 == chunk:
-                    gram(recv, coherence, i, looks)
-    with jax.named_scope("link"):
-        vec_real, vec_imag = link(coherence, WINDOWS)
+            for i in members:
+                gram(recv, coherence, i, looks)
+        with jax.named_scope("link"):
+            linked.append(link(coherence, members))
+    vec_real, vec_imag = [
+        jnp.concatenate([linked[0][c][:4], linked[1][c][:4], linked[0][c][4:], linked[1][c][4:]], axis=0) for c in range(2)
+    ]
 
     with jax.named_scope("note"):
         rows = jnp.concatenate([vec_real] + [vec_imag] * 4 + [vec_real] * 3, axis=0)
@@ -269,11 +338,12 @@
                 pltpu.VMEM((TILES, n, dates, 128), BF16),
                 pltpu.VMEM((128, 128), F32),
                 pltpu.VMEM((n, 2, 128), F32),
-                pltpu.SemaphoreType.DMA((LOADS, 3)),
+                pltpu.SemaphoreType.DMA((LOADS, 2)),
                 pltpu.SemaphoreType.DMA((1,)),
                 pltpu.SemaphoreType.DMA((2, n)),
                 pltpu.SemaphoreType.DMA((1,)),
                 pltpu.SemaphoreType.DMA((n,)),
+                pltpu.SemaphoreType.REGULAR((n,)),
             ],
             compiler_params=pltpu.CompilerParams(collective_id=0, has_side_effects=True),
         )(slc, usable)

time: 95 us -> 84.7 us (0.89)
  Pallas kernels: 94.2 us -> 83.7 us
    pallas_call x1, Pallas kernels: 93.1 us -> 82.6 us  [step(): pl.pallas_call(functools.partial(kernel, n), out_shape=(pltpu.VMEM(cohere...]
where the time goes in v4:
time: 84.7 us; the launch traced here: 84.4 us
  Pallas kernels  83.7 us (99%)
    pallas_call x1, Pallas kernels, step(): pl.pallas_call(functools.partial(kernel, n), out_shape=(pltpu.VMEM(cohere...  82.6 us

profile of v4, /device:TPU:65, one launch (start us, length us, event | category | flops | bytes accessed | tf_op | source)
XLA Modules:
  0.0 84.4 jit_solution(16446023133003973538)
XLA Ops:
  0.6 82.6 %shard_map.41 = (bf16[2,1,1,16,128,128]{5,4,3,2,1,0:T(8,128)(2,1)S(1)}, f32[16,2,128]{2,1,0:T(2,128)S(1)}) custom-call(bf16[2,100,8,256]{3,2,1,0:T(8,128)(2,1)} %slc_hbm.1, s32[100,8,256]{2,1,0:T(8,128)} %usable_hbm.1), custom_call_target="tpu_custom_call" | custom-call | tf_op jit(solution)/shard_map/pallas_call | solution.py:326
  83.3 1.1 %shard_map.42 = (bf16[2,1,1,16,128,128]{5,4,3,2,1,0:T(8,128)(2,1)}, f32[2,8,256]{2,1,0:T(8,128)}) custom-call(bf16[2,1,1,16,128,128]{5,4,3,2,1,0:T(8,128)(2,1)S(1)} %get-tuple-element.4.coherence, f32[16,2,128]{2,1,0:T(2,128)S(1)} %get-tuple-element.5.notes), custom_call_target="tpu_custom_call" | custom-call | tf_op jit(solution)/shard_map/pallas_call | solution.py:350

commit v5 on v4

--- a/solution.py
+++ b/solution.py
@@ -12,22 +12,25 @@
 F32, BF16 = jnp.float32, jnp.bfloat16
 WINDOWS = 16
 LATE = 3
+SPLIT = 4
 LOADS = 5
-CHUNKS = ((0, 13), (13, 12))
+PAIRS = (SPLIT, 8 - SPLIT)
+REST = 3 * SPLIT
 TILES = 25
-REST = 12
+CHUNKS = ((0, REST + 1), (REST + 1, TILES - REST - 1))
 
 
 def places(i):
-    chunk, spot = divmod(i % 8, 4)
-    return CHUNKS[chunk][0] + 4 * (i // 8) + spot, CHUNKS[chunk][0] + 8 + spot
+    chunk = int(i % 8 >= SPLIT)
+    spot = CHUNKS[chunk][0] + i % 8 - chunk * SPLIT
+    return chunk, spot + PAIRS[chunk] * (i // 8), spot + 2 * PAIRS[chunk]
 
 
 def lane_iota(shape):
     return lax.broadcasted_iota(jnp.int32, shape, len(shape) - 1)
 
 
-def pack(slc_ref, usable_ref, plane, split1, split2, send, loads, between, looks, dates, blocks):
+def pack(slc_ref, usable_ref, plane, split1, split2, send, loads, between, ready, looks, dates):
     rows = looks * dates
     step = looks // LOADS
 
@@ -44,8 +47,17 @@
         for piece, copies in enumerate(loads):
             for copy in copies:
                 copy.wait()
-            lax.fori_loop(piece * step, piece * step + step, mask_step, 0, unroll=4)
+            lax.fori_loop(piece * step, piece * step + step, mask_step, 0, unroll=20)
     between()
+
+    def out_step(b, carry):
+        one = split1[pl.ds(pl.multiple_of(b * 128, 128), 128), :].reshape(16, 8, 128).astype(BF16)
+        two = split2[pl.ds(pl.multiple_of(b * 64, 64), 64), :].reshape(8, 8, 128).astype(BF16)
+        for (base, _), count, at in zip(CHUNKS, PAIRS, (0, SPLIT)):
+            send[b, base:base + count] = one[at:at + count]
+            send[b, base + count:base + 2 * count] = one[8 + at:8 + at + count]
+            send[b, base + 2 * count:base + 3 * count] = two[at:at + count]
+        return carry
 
     bit = (lane_iota((8, 8, 128)) // 8) % 2 == 1
     groups = [(c, r) for c in range(2) for r in range(4)]
@@ -67,7 +79,7 @@
             split2[pl.ds(half * 512 + a, 64, stride=8), :] = pairs
             return carry
 
-        lax.fori_loop(0, dates, date_step, 0, unroll=4)
+        lax.fori_loop(0, dates, date_step, 0, unroll=8)
 
         left = [plane[half, c * rows + (96 + r) * dates:c * rows + (97 + r) * dates, :] for c, r in groups]
         for b in range(8):
@@ -78,33 +90,23 @@
                 tile = jnp.where(lane_iota((8, 128)) // 16 == g, moved, tile)
             send[half * 8 + b, REST] = tile.astype(BF16)
 
-    def out_step(b, carry):
-        one = split1[pl.ds(pl.multiple_of(b * 128, 128), 128), :].reshape(16, 8, 128).astype(BF16)
-        two = split2[pl.ds(pl.multiple_of(b * 64, 64), 64), :].reshape(8, 8, 128).astype(BF16)
-        for chunk, (base, _) in enumerate(CHUNKS):
-            send[b, base:base + 4] = one[4 * chunk:4 * chunk + 4]
-            send[b, base + 4:base + 8] = one[8 + 4 * chunk:12 + 4 * chunk]
-            send[b, base + 8:base + 12] = two[4 * chunk:4 * chunk + 4]
-        return carry
-
-    with jax.named_scope("cast"):
-        lax.fori_loop(0, blocks, out_step, 0)
+        lax.fori_loop(8 * half, 8 * half + 8, out_step, 0)
+        ready(half)
 
 
 def gram(recv, coherence, i, looks):
     lane = lane_iota((128, 128))
-    own, shared = places(i)
+    _, own, shared = places(i)
     one = recv[own].astype(F32).reshape(128, 128)
     pair = recv[shared].astype(F32).reshape(128, 128)
     rest = recv[REST].astype(F32).reshape(128, 128)
     in_pair = ((lane // 8) % 2 == 1) == (i < 8)
     two = jnp.where(in_pair, pair, jnp.where(lane % 16 == i, rest, 0.0))
-    sign = jnp.where(lane < 64, 1.0, -1.0)
     plain = jnp.concatenate([one, two], axis=1).astype(BF16)
-    turned = jnp.concatenate([pltpu.roll(one, 64, 1) * sign, pltpu.roll(two, 64, 1) * sign], axis=1).astype(BF16)
-    both = jnp.concatenate([plain, turned], axis=0)
-    cross = lax.dot_general(both, plain, (((1,), (1,)), ((), ())), preferred_element_type=F32)
-    real, imag = cross[:128], cross[128:]
+    turned = jnp.concatenate([one.T, two.T], axis=0)
+    swapped = jnp.concatenate([-turned[64:128], turned[:64], -turned[192:], turned[128:192]], axis=0)
+    cross = jnp.dot(plain, jnp.concatenate([turned, swapped], axis=1).astype(BF16), preferred_element_type=F32)
+    real, imag = cross[:, :128], cross[:, 128:]
     eye = lax.broadcasted_iota(jnp.int32, (128, 128), 0) == lane
     diagonal = jnp.where(eye, real, 0.0)
     column = lax.rsqrt(jnp.sum(diagonal, axis=1, keepdims=True) * (1.0 / looks) + 1e-05)
@@ -115,8 +117,8 @@
 
 
 def link(coherence, members):
-    windows = len(members)
-    row = lax.broadcasted_iota(jnp.int32, (4 * windows, 256), 0) % windows
+    windows = -(-len(members) // 8) * 8
+    row = lax.broadcasted_iota(jnp.int32, (4 * windows, 128), 0) % windows
     real, imag = jnp.ones((windows, 128), F32), jnp.zeros((windows, 128), F32)
     scale = None
     for step in range(ITERS):
@@ -131,10 +133,14 @@
             ],
             axis=0,
         )
+        lhs = lhs.astype(BF16)
         total = jnp.zeros((4 * windows, 128), F32)
-        for w, i in enumerate(members):
-            stacked = jnp.concatenate([coherence[0, 0, 0, i], coherence[1, 0, 0, i]], axis=0)
-            total += jnp.dot(jnp.where(row == w, lhs, 0.0).astype(BF16), stacked, preferred_element_type=F32)
+        for w in range(0, len(members), 2):
+            matrices = jnp.concatenate(
+                [jnp.concatenate([coherence[c, 0, 0, i] for c in range(2)], axis=0) for i in members[w:w + 2]], axis=1
+            )
+            product = jnp.dot(lhs, matrices, preferred_element_type=F32)
+            total = jnp.where(row == w, product[:, :128], jnp.where(row == w + 1, product[:, 128:], total))
         real = total[:windows] + total[windows:2 * windows]
         imag = total[2 * windows:3 * windows] + total[3 * windows:]
         if scale is not None:
@@ -192,9 +198,6 @@
             def _():
                 pl.semaphore_signal(known_sem.at[me], inc=1, device_id={"date": to}, device_id_type=MESH)
 
-    pl.when(me > 0)(enter)
-    pack(slc_ref, usable_ref, plane, split1, split2, send, loads, lambda: pl.when(first)(enter), looks, dates, n)
-
     def sample_copy(chunk, to, source):
         tiles = pl.ds(*CHUNKS[chunk])
         return pltpu.make_async_remote_copy(
@@ -202,19 +205,29 @@
             device_id={"date": to}, device_id_type=MESH,
         )
 
-    def send_lower(chunk):
+    def ready(half):
         for k in order:
             to = lax.rem(me + k, n)
 
+            @pl.when((rank_of(to) < rank) & (to // (n // 2) == half))
+            def _():
+                sample_copy(0, to, me).start()
+
+    pl.when(me > 0)(enter)
+    pack(slc_ref, usable_ref, plane, split1, split2, send, loads, lambda: pl.when(first)(enter), ready, looks, dates)
+
+    def send_lower():
+        for k in order:
+            to = lax.rem(me + k, n)
+
             @pl.when(rank_of(to) < rank)
             def _():
-                sample_copy(chunk, to, me).start()
+                sample_copy(1, to, me).start()
 
     late = n - LATE
     entry = [*range(1, n - 1), 0, n - 1]
     with jax.named_scope("start"):
-        send_lower(0)
-        pl.when(rank < late)(lambda: send_lower(1))
+        pl.when(rank < late)(send_lower)
         recv[:, me] = send[me]
         for place, z in enumerate(entry):
 
@@ -229,7 +242,7 @@
             pl.semaphore_signal(known_sem.at[0], inc=1, device_id={"date": n - 1}, device_id_type=MESH)
             pl.semaphore_signal(known_sem.at[n - 1], inc=1, device_id={"date": 0}, device_id_type=MESH)
 
-        pl.when(rank >= late)(lambda: send_lower(1))
+        pl.when(rank >= late)(send_lower)
         for z in entry[late:]:
 
             @pl.when(rank < rank_of(z))
@@ -250,19 +263,20 @@
             for k in order:
                 source = lax.rem(me + n - k, n)
                 sample_copy(chunk, source, source).wait_recv()
-        members = [i for i in range(WINDOWS) if (i % 8) // 4 == chunk]
+        members = [i for i in range(WINDOWS) if places(i)[0] == chunk]
         with jax.named_scope("gram"):
             for i in members:
                 gram(recv, coherence, i, looks)
         with jax.named_scope("link"):
             linked.append(link(coherence, members))
     vec_real, vec_imag = [
-        jnp.concatenate([linked[0][c][:4], linked[1][c][:4], linked[0][c][4:], linked[1][c][4:]], axis=0) for c in range(2)
+        jnp.concatenate([linked[chunk][c][half * PAIRS[chunk]:][:PAIRS[chunk]] for half in range(2) for chunk in range(2)], axis=0)
+        for c in range(2)
     ]
 
     with jax.named_scope("note"):
         rows = jnp.concatenate([vec_real] + [vec_imag] * 4 + [vec_real] * 3, axis=0)
-        turn[...] = rows.T
+        turn[0:128] = rows.T
         lane = lane_iota((2 * n, 128))
         message = jnp.zeros((2 * n, 128), F32)
         for q in range(4):
@@ -282,14 +296,13 @@
             note_copy(k).start()
         notes[me] = note[me]
         pltpu.make_async_copy(send.at[0:n - 1], send.at[0:n - 1], send_sem.at[0]).wait()
+        pltpu.make_async_copy(note.at[0:n - 1], note.at[0:n - 1], note_send.at[0]).wait()
         for k in order:
             source = lax.rem(me + n - k, n)
             pltpu.make_async_remote_copy(
                 src_ref=note.at[source], dst_ref=notes.at[source], send_sem=note_send.at[0], recv_sem=note_recv.at[k],
                 device_id={"date": source}, device_id_type=MESH,
             ).wait_recv()
-
-    pltpu.make_async_copy(note.at[0:n - 1], note.at[0:n - 1], note_send.at[0]).wait()
 
 
 def store(coherence, notes, coherence_out, linked_out, linked, sem):
@@ -331,12 +344,12 @@
             scratch_shapes=[
                 pltpu.VMEM(slc.shape, BF16),
                 pltpu.VMEM(usable.shape, jnp.int32),
-                pltpu.VMEM((windows // 128, rows, 128), F32),
-                pltpu.VMEM((windows * dates, 128), F32),
-                pltpu.VMEM((windows * dates // 2, 128), F32),
+                pltpu.VMEM((windows // 128, rows + 8, 128), F32),
+                pltpu.VMEM((windows * dates + 8, 128), F32),
+                pltpu.VMEM((windows * dates // 2 + 8, 128), F32),
                 pltpu.VMEM((n, TILES, dates, 128), BF16),
                 pltpu.VMEM((TILES, n, dates, 128), BF16),
-                pltpu.VMEM((128, 128), F32),
+                pltpu.VMEM((136, 128), F32),
                 pltpu.VMEM((n, 2, 128), F32),
                 pltpu.SemaphoreType.DMA((LOADS, 2)),
                 pltpu.SemaphoreType.DMA((1,)),

time: 84.7 us -> 84.4 us (level)
  no operation moved by 1% of the time
where the time goes in v5:
time: 84.4 us; the launch traced here: 83.7 us
  Pallas kernels  83.1 us (98%)
    pallas_call x1, Pallas kernels, step(): pl.pallas_call(functools.partial(kernel, n), out_shape=(pltpu.VMEM(cohere...  82 us

profile of v5, /device:TPU:65, one launch (start us, length us, event | category | flops | bytes accessed | tf_op | source)
XLA Modules:
  0.0 83.7 jit_solution(10662596901335049509)
XLA Ops:
  0.6 82.0 %shard_map.41 = (bf16[2,1,1,16,128,128]{5,4,3,2,1,0:T(8,128)(2,1)S(1)}, f32[16,2,128]{2,1,0:T(2,128)S(1)}) custom-call(bf16[2,100,8,256]{3,2,1,0:T(8,128)(2,1)} %slc_hbm.1, s32[100,8,256]{2,1,0:T(8,128)} %usable_hbm.1), custom_call_target="tpu_custom_call" | custom-call | tf_op jit(solution)/shard_map/pallas_call | solution.py:339
  82.6 1.1 %shard_map.42 = (bf16[2,1,1,16,128,128]{5,4,3,2,1,0:T(8,128)(2,1)}, f32[2,8,256]{2,1,0:T(8,128)}) custom-call(bf16[2,1,1,16,128,128]{5,4,3,2,1,0:T(8,128)(2,1)S(1)} %get-tuple-element.4.coherence, f32[16,2,128]{2,1,0:T(2,128)S(1)} %get-tuple-element.5.notes), custom_call_target="tpu_custom_call" | custom-call | tf_op jit(solution)/shard_map/pallas_call | solution.py:363

commit v6 on v5

--- a/solution.py
+++ b/solution.py
@@ -112,16 +112,20 @@
     column = lax.rsqrt(jnp.sum(diagonal, axis=1, keepdims=True) * (1.0 / looks) + 1e-05)
     row = lax.rsqrt(jnp.sum(diagonal, axis=0, keepdims=True) * (1.0 / looks) + 1e-05)
     factor = column * row * (1.0 / looks)
-    coherence[0, 0, 0, i] = (real * factor).astype(BF16)
-    coherence[1, 0, 0, i] = (imag * factor).astype(BF16)
-
-
-def link(coherence, members):
+    rounded = [(real * factor).astype(BF16), (imag * factor).astype(BF16)]
+    for c in range(2):
+        coherence[c, 0, 0, i] = rounded[c]
+    return [jnp.sum(part.astype(F32), axis=0, keepdims=True) for part in rounded]
+
+
+def link(coherence, members, sums):
     windows = -(-len(members) // 8) * 8
     row = lax.broadcasted_iota(jnp.int32, (4 * windows, 128), 0) % windows
-    real, imag = jnp.ones((windows, 128), F32), jnp.zeros((windows, 128), F32)
-    scale = None
-    for step in range(ITERS):
+    assert windows == len(members)
+    real = jnp.concatenate([pair[0] for pair in sums], axis=0)
+    imag = -jnp.concatenate([pair[1] for pair in sums], axis=0)
+    scale = lax.rsqrt(jnp.sum(real * real + imag * imag, axis=1, keepdims=True) * (1.0 / 128) + 1e-05)
+    for step in range(1, ITERS):
         high_real, high_imag = real.astype(BF16).astype(F32), imag.astype(BF16).astype(F32)
         low_real, low_imag = real - high_real, imag - high_imag
         lhs = jnp.concatenate(
@@ -143,8 +147,7 @@
             total = jnp.where(row == w, product[:, :128], jnp.where(row == w + 1, product[:, 128:], total))
         real = total[:windows] + total[windows:2 * windows]
         imag = total[2 * windows:3 * windows] + total[3 * windows:]
-        if scale is not None:
-            real, imag = real * scale, imag * scale
+        real, imag = real * scale, imag * scale
         scale = lax.rsqrt(jnp.sum(real * real + imag * imag, axis=1, keepdims=True) * (1.0 / 128) + 1e-05)
     return real * scale, imag * scale
 
@@ -265,10 +268,9 @@
                 sample_copy(chunk, source, source).wait_recv()
         members = [i for i in range(WINDOWS) if places(i)[0] == chunk]
         with jax.named_scope("gram"):
-            for i in members:
-                gram(recv, coherence, i, looks)
+            sums = [gram(recv, coherence, i, looks) for i in members]
         with jax.named_scope("link"):
-            linked.append(link(coherence, members))
+            linked.append(link(coherence, members, sums))
     vec_real, vec_imag = [
         jnp.concatenate([linked[chunk][c][half * PAIRS[chunk]:][:PAIRS[chunk]] for half in range(2) for chunk in range(2)], axis=0)
         for c in range(2)

time: 84.4 us -> 84.3 us (level)
  no operation moved by 1% of the time
where the time goes in v6:
time: 84.3 us; the launch traced here: 83.6 us
  Pallas kernels  83 us (98%)
    pallas_call x1, Pallas kernels, step(): pl.pallas_call(functools.partial(kernel, n), out_shape=(pltpu.VMEM(cohere...  81.9 us

profile of v6, /device:TPU:65, one launch (start us, length us, event | category | flops | bytes accessed | tf_op | source)
XLA Modules:
  0.0 83.6 jit_solution(452905171475942679)
XLA Ops:
  0.6 81.9 %shard_map.41 = (bf16[2,1,1,16,128,128]{5,4,3,2,1,0:T(8,128)(2,1)S(1)}, f32[16,2,128]{2,1,0:T(2,128)S(1)}) custom-call(bf16[2,100,8,256]{3,2,1,0:T(8,128)(2,1)} %slc_hbm.1, s32[100,8,256]{2,1,0:T(8,128)} %usable_hbm.1), custom_call_target="tpu_custom_call" | custom-call | tf_op jit(solution)/shard_map/pallas_call | solution.py:341
  82.5 1.1 %shard_map.42 = (bf16[2,1,1,16,128,128]{5,4,3,2,1,0:T(8,128)(2,1)}, f32[2,8,256]{2,1,0:T(8,128)}) custom-call(bf16[2,1,1,16,128,128]{5,4,3,2,1,0:T(8,128)(2,1)S(1)} %get-tuple-element.4.coherence, f32[16,2,128]{2,1,0:T(2,128)S(1)} %get-tuple-element.5.notes), custom_call_target="tpu_custom_call" | custom-call | tf_op jit(solution)/shard_map/pallas_call | solution.py:365
